TPU v7x, 32 devices: a whole 2x2x4 slice. The times are simulated.
32 devices in a mesh: scen: 16 (over z, y, x), fac: 2 (over core).
Axes of the slice: x: 2, y: 2, z: 4, core: 2. Of those that a mesh axis runs over, the one named last changes fastest.
Arguments:
- scenarios: bfloat16 [256, 8192], P(('scen', 'fac')), may hold values from -40 to 40
Outputs:
- shrunk: float32 [8192, 8192], P('scen', 'fac')
- shrinkage: float32 [], replicated
- col_mean: float32 [8192], P('fac')
All inputs are finite; a program needn't handle non-finite values.
Results may differ from a plain program's by a relative error of at most 0.0008.
Values may be sent and summed in bfloat16 or wider, within the bound.
A program may use at most 64 MiB of HBM per device.

v0:
```python
import jax
import jax.numpy as jnp
from jax import lax
from jax.sharding import PartitionSpec as P


def on_device(scenarios):
    row_count = scenarios.shape[0]
    factors = scenarios.shape[1]
    scen_size = lax.axis_size("scen")
    fac_size = lax.axis_size("fac")
    total_rows = row_count * scen_size * fac_size
    group_width = factors // scen_size
    block_width = factors // fac_size
    owner_idx = lax.axis_index("scen")
    block_idx = lax.axis_index("fac")
    col_total = lax.psum(jnp.sum(scenarios.astype(jnp.float32), axis=0), ("scen", "fac"))
    col_mean = col_total / total_rows
    centered = (scenarios.astype(jnp.float32) - col_mean).astype(jnp.bfloat16)
    as_float = centered.astype(jnp.float32)
    squared = jnp.sum(as_float * as_float, axis=1)
    trace_part = jnp.sum(squared)
    fourth_part = jnp.sum(squared * squared)
    trace_total, fourth_total = lax.psum((trace_part, fourth_part), ("scen", "fac"))
    contract = (((0,), (0,)), ((), ()))
    local_rows = lax.all_gather(centered, "fac", axis=0, tiled=True)
    narrow_all = lax.all_to_all(local_rows, "scen", split_axis=1, concat_axis=0, tiled=True)
    wide_cols = lax.dynamic_slice_in_dim(local_rows, block_idx * block_width, block_width, 1)
    summed = lax.dot_general(
        narrow_all,
        lax.all_gather(wide_cols, "scen", axis=0, tiled=True),
        contract,
        preferred_element_type=jnp.float32,
    )
    covariance = summed / total_rows
    row_index = owner_idx * group_width + lax.broadcasted_iota(
        jnp.int32, (group_width, block_width), 0
    )
    col_index = block_idx * block_width + lax.broadcasted_iota(
        jnp.int32, (group_width, block_width), 1
    )
    diag_mask = (row_index == col_index).astype(jnp.float32)
    mu_scale = trace_total / (total_rows * factors)
    distance = covariance - mu_scale * diag_mask
    frob_sum = lax.psum(jnp.sum(distance * distance), ("scen", "fac"))
    spread = frob_sum / factors
    norm_sq = factors * (spread + mu_scale * mu_scale)
    beta_value = (fourth_total / total_rows - norm_sq) / (factors * total_rows)
    shrinkage = beta_value / spread
    shrunk = (1.0 - shrinkage) * covariance + shrinkage * mu_scale * diag_mask
    mean_block = lax.dynamic_slice_in_dim(col_mean, block_idx * block_width, block_width, 0)
    return (shrunk, shrinkage, mean_block)


def solution(mesh):
    return jax.shard_map(
        on_device,
        mesh=mesh,
        in_specs=(P(("scen", "fac"), None),),
        out_specs=(P("scen", "fac"), P(), P("fac")),
        check_vma=False,
    )
```

profile of v0, /device:TPU:0, one launch (start us, length us, event | category | flops | bytes accessed | tf_op | source)
XLA Modules:
  0.0 179.8 jit_solution(12894808986534440513)
XLA Ops:
  7.2 0.0 all-gather.2.cloned.1.call-start
  7.2 1.0 convert_reduce_fusion
  8.2 42.1 %psum.28 = f32[8192]{0:T(1024)S(1)} all-reduce(f32[8192]{0:T(1024)S(1)} %convert_reduce_fusion), channel_id=1, replica_groups=mesh['scen'=16,'fac'=2] {'scen','fac'}, use_global_device_ids=true, to_apply=%region_1.0 | all-reduce | flops 8192 | bytes 65536 | tf_op jit(solution)/shard_map/psum | solution.py:17
  50.4 1.6 fusion.5
  52.0 2.0 %all_gather.6 = bf16[16,8192]{1,0:T(8,128)(2,1)S(1)} all-gather(bf16[8,8192]{1,0:T(8,128)(2,1)S(1)} %get-tuple-element.7), channel_id=1, replica_groups=mesh['scen'=16,'fac'=2] {'fac'}, dimensions={0}, use_global_device_ids=true | all-gather | bytes 393216 | tf_op jit(solution)/shard_map/all_gather | solution.py:26
  54.0 0.7 constant_dynamic-slice_fusion
  54.6 0.0 all-gather.2.cloned.1.call-update
  54.6 0.7 copy.8
  55.4 5.4 %all-to-all-start = ((bf16[16,16,512]{2,0,1:T(8,128)(2,1)}), bf16[16,16,512]{2,0,1:T(8,128)(2,1)S(1)}, u32[]{:S(2)}, u32[]{:S(2)}) async-start(bf16[16,16,512]{2,0,1:T(8,128)(2,1)} %bitcast.8), calls=%async_computation | async-start | bytes 524288 | tf_op jit(solution)/shard_map/all_to_all | solution.py:27
  60.8 41.2 %psum.30 = f32[]{:T(128)} all-reduce(f32[]{:T(128)} %get-tuple-element.3), channel_id=1, replica_groups=mesh['scen'=16,'fac'=2] {'scen','fac'}, use_global_device_ids=true, to_apply=%region_6.0 | all-reduce | flops 1 | bytes 8 | tf_op jit(solution)/shard_map/psum | solution.py:24
  102.0 0.6 dynamic_slice.7
  104.6 0.7 multiply_reduce_fusion
  105.2 0.0 all-to-all-done
  105.2 10.7 %all-gather.2.cloned.1.call-done = bf16[256,4096]{1,0:T(8,128)(2,1)} async-done(((bf16[16,4096]{1,0:T(8,128)(2,1)}), bf16[256,4096]{1,0:T(8,128)(2,1)}) %all-gather.2.cloned.1.call-update) | async-done | bytes 2097168 | tf_op jit(solution)/shard_map/all_gather | solution.py:31
  115.9 6.8 %fusion.2 = (f32[]{:T(128)}, f32[512,4096]{1,0:T(8,128)}) fusion(f32[]{:T(128)S(6)} %div.32, s32[4096]{0:T(1024)S(1)} %iota_add_fusion, s32[512]{0:T(512)S(1)} %iota_add_fusion.1, bf16[256,512]{1,0:T(8,128)(2,1)S(1)} %bitcast.10, bf16[256,4096]{1,0:T(8,128)(2,1)} %all-gather.2.cloned.1.call-done), kind=kOutput, calls=%fused_computation.4 | convolution fusion | flops 1086324736 | bytes 10766344 | tf_op jit(solution)/shard_map/dot_general | solution.py:29
  122.8 39.0 %all-reduce = (f32[]{:T(128)}, f32[]{:T(128)}) all-reduce(f32[]{:T(128)} %multiply_reduce_fusion, f32[]{:T(128)} %get-tuple-element.8), channel_id=1, replica_groups=mesh['scen'=16,'fac'=2] {'scen','fac'}, use_global_device_ids=true, to_apply=%region_4.0 | all-reduce | flops 2 | bytes 16 | tf_op jit(solution)/shard_map/psum | solution.py:24
  163.1 8.7 %fusion.3 = f32[512,4096]{1,0:T(8,128)} fusion(f32[512,4096]{1,0:T(8,128)} %get-tuple-element.9, f32[]{:T(128)S(6)} %mul.61, f32[]{:T(128)S(6)} %mul.58, s32[4096]{0:T(1024)S(1)} %iota_add_fusion, s32[512]{0:T(512)S(1)} %iota_add_fusion.1), kind=kLoop, calls=%fused_computation.5 | loop fusion | flops 8388608 | bytes 16795656 | tf_op jit(solution)/shard_map/add | solution.py:50
  (3 shorter events, 0.0 us)
Async XLA Ops:
  7.2 108.7 %all-gather.2.cloned.1.call-start = ((), (), s32[]{:S(2)}) async-start(), calls=%async_computation.1 | async-start | bytes 2228224 | tf_op jit(solution)/shard_map/all_gather | solution.py:31
  55.4 49.9 %all-to-all-start = ((bf16[16,16,512]{2,0,1:T(8,128)(2,1)}), bf16[16,16,512]{2,0,1:T(8,128)(2,1)S(1)}, u32[]{:S(2)}, u32[]{:S(2)}) async-start(bf16[16,16,512]{2,0,1:T(8,128)(2,1)} %bitcast.8), calls=%async_computation | async-start | bytes 524288 | tf_op jit(solution)/shard_map/all_to_all | solution.py:27
Sparse Core Ops, SparseCore 0:
  54.8 61.1 all-gather.1
where the time goes:
time: 181 us; the launch traced here: 180 us
  blocking collectives  124 us (69%)
  between operations  18.5 us (10%)
  other arithmetic  12 us (7%)
  waiting for transfers between devices  10.7 us (6%)
  matrix products  6.84 us (4%)
  starting transfers between devices  5.46 us (3%)
  local copies, waits for them, and re-layouts  2 us (1%)
    psum x2, blocking collectives, on_device(): lax.psum((trace_part, fourth_part), ('scen', 'fac'))  80.2 us
    psum x1, blocking collectives, on_device(): lax.psum(jnp.sum(scenarios.astype(jnp.float32), axis=0), ('scen', 'fac'))  42.1 us
    all_gather x1, waiting for transfers between devices, on_device(): lax.all_gather(wide_cols, 'scen', axis=0, tiled=True)  10.7 us
    add x1, other arithmetic, on_device(): shrunk = (1.0 - shrinkage) * covariance + shrinkage * mu_scale * diag_mask  8.69 us
    dot_general x1, matrix products, on_device(): lax.dot_general(narrow_all, lax.all_gather(wide_cols, 'scen', axis=0, til...  6.84 us
    all_to_all x1, starting transfers between devices, on_device(): lax.all_to_all(local_rows, 'scen', split_axis=1, concat_axis=0, tiled=True)  5.42 us
  transfers between devices with their start and end apart: 2, of which 1 were waited for; matrix products, arithmetic and copies ran while one was open for 1% of the time, Pallas kernels for 0%

commit v1 on v0

--- a/solution.py
+++ b/solution.py
@@ -14,7 +14,8 @@
     block_width = factors // fac_size
     owner_idx = lax.axis_index("scen")
     block_idx = lax.axis_index("fac")
-    col_total = lax.psum(jnp.sum(scenarios.astype(jnp.float32), axis=0), ("scen", "fac"))
+    inner = lax.psum(jnp.sum(scenarios.astype(jnp.float32), axis=0), "fac")
+    col_total = lax.psum(inner, "scen")
     col_mean = col_total / total_rows
     centered = (scenarios.astype(jnp.float32) - col_mean).astype(jnp.bfloat16)
     as_float = centered.astype(jnp.float32)

time: 181 us -> 217 us (1.20)
  blocking collectives: 124 us -> 164 us
    psum x1 -> x2, blocking collectives: 42.1 us -> 82 us  [the longest x1 78.2 us: on_device(): col_total = lax.psum(inner, 'scen')]
where the time goes in v1:
time: 217 us
  blocking collectives  164 us (76%)
  between operations  18.5 us (9%)
  other arithmetic  12 us (6%)
  waiting for transfers between devices  9.5 us (4%)
  matrix products  6.85 us (3%)
  starting transfers between devices  3.57 us (2%)
    psum x2, blocking collectives, on_device(): lax.psum((trace_part, fourth_part), ('scen', 'fac'))  80.4 us
    psum x1, blocking collectives, on_device(): col_total = lax.psum(inner, 'scen')  78.2 us
    all_gather x1, waiting for transfers between devices, on_device(): lax.all_gather(wide_cols, 'scen', axis=0, tiled=True)  9.48 us
    add x1, other arithmetic, on_device(): shrunk = (1.0 - shrinkage) * covariance + shrinkage * mu_scale * diag_mask  8.69 us
    dot_general x1, matrix products, on_device(): lax.dot_general(narrow_all, lax.all_gather(wide_cols, 'scen', axis=0, til...  6.85 us
  transfers between devices with their start and end apart: 2, of which 1 were waited for; matrix products, arithmetic and copies ran while one was open for 1% of the time, Pallas kernels for 0%

profile of v1, /device:TPU:0, one launch (start us, length us, event | category | flops | bytes accessed | tf_op | source)
XLA Modules:
  0.0 216.8 jit_solution(9123366329811911607)
XLA Ops:
  7.2 0.0 all-gather.2.cloned.1.call-start
  7.2 1.0 convert_reduce_fusion
  8.2 3.7 %psum.35 = f32[8192]{0:T(1024)S(1)} all-reduce(f32[8192]{0:T(1024)S(1)} %convert_reduce_fusion), channel_id=1, replica_groups=mesh['scen'=16,'fac'=2] {'fac'}, use_global_device_ids=true, to_apply=%region_1.0 | all-reduce | flops 8192 | bytes 65536 | tf_op jit(solution)/shard_map/psum | solution.py:17
  11.9 78.2 %psum.36 = f32[8192]{0:T(1024)S(1)} all-reduce(f32[8192]{0:T(1024)S(1)} %psum.35), channel_id=1, replica_groups=mesh['scen'=16,'fac'=2] {'scen'}, use_global_device_ids=true, to_apply=%region_2.0 | all-reduce | flops 8192 | bytes 65536 | tf_op jit(solution)/shard_map/psum | solution.py:18
  90.2 1.6 fusion.5
  91.8 2.0 all_gather.6
  93.8 0.7 constant_dynamic-slice_fusion
  94.5 0.0 all-gather.2.cloned.1.call-update
  94.5 0.7 copy.8
  95.2 3.5 %all-to-all-start = ((bf16[16,16,512]{2,0,1:T(8,128)(2,1)}), bf16[16,16,512]{2,0,1:T(8,128)(2,1)S(1)}, u32[]{:S(2)}, u32[]{:S(2)}) async-start(bf16[16,16,512]{2,0,1:T(8,128)(2,1)} %bitcast.8), calls=%async_computation | async-start | bytes 524288 | tf_op jit(solution)/shard_map/all_to_all | solution.py:28
  98.8 41.1 %psum.38 = f32[]{:T(128)} all-reduce(f32[]{:T(128)} %get-tuple-element.3), channel_id=1, replica_groups=mesh['scen'=16,'fac'=2] {'scen','fac'}, use_global_device_ids=true, to_apply=%region_7.0 | all-reduce | flops 1 | bytes 8 | tf_op jit(solution)/shard_map/psum | solution.py:25
  139.8 0.6 dynamic_slice.7
  142.4 0.7 multiply_reduce_fusion
  143.1 0.0 all-to-all-done
  143.1 9.5 %all-gather.2.cloned.1.call-done = bf16[256,4096]{1,0:T(8,128)(2,1)} async-done(((bf16[16,4096]{1,0:T(8,128)(2,1)}), bf16[256,4096]{1,0:T(8,128)(2,1)}) %all-gather.2.cloned.1.call-update) | async-done | bytes 2097168 | tf_op jit(solution)/shard_map/all_gather | solution.py:32
  152.5 6.9 %fusion.2 = (f32[]{:T(128)}, f32[512,4096]{1,0:T(8,128)}) fusion(f32[]{:T(128)S(6)} %div.32, s32[4096]{0:T(1024)S(1)} %iota_add_fusion, s32[512]{0:T(512)S(1)} %iota_add_fusion.1, bf16[256,512]{1,0:T(8,128)(2,1)S(1)} %bitcast.10, bf16[256,4096]{1,0:T(8,128)(2,1)} %all-gather.2.cloned.1.call-done), kind=kOutput, calls=%fused_computation.4 | convolution fusion | flops 1086324736 | bytes 10766344 | tf_op jit(solution)/shard_map/dot_general | solution.py:30
  159.4 39.3 %all-reduce = (f32[]{:T(128)}, f32[]{:T(128)}) all-reduce(f32[]{:T(128)} %multiply_reduce_fusion, f32[]{:T(128)} %get-tuple-element.8), channel_id=1, replica_groups=mesh['scen'=16,'fac'=2] {'scen','fac'}, use_global_device_ids=true, to_apply=%region_5.0 | all-reduce | flops 2 | bytes 16 | tf_op jit(solution)/shard_map/psum | solution.py:25
  200.1 8.7 %fusion.3 = f32[512,4096]{1,0:T(8,128)} fusion(f32[512,4096]{1,0:T(8,128)} %get-tuple-element.9, f32[]{:T(128)S(6)} %mul.61, f32[]{:T(128)S(6)} %mul.58, s32[4096]{0:T(1024)S(1)} %iota_add_fusion, s32[512]{0:T(512)S(1)} %iota_add_fusion.1), kind=kLoop, calls=%fused_computation.5 | loop fusion | flops 8388608 | bytes 16795656 | tf_op jit(solution)/shard_map/add | solution.py:51
  (3 shorter events, 0.0 us)
Async XLA Ops:
  7.2 145.4 %all-gather.2.cloned.1.call-start = ((), (), s32[]{:S(2)}) async-start(), calls=%async_computation.1 | async-start | bytes 2228224 | tf_op jit(solution)/shard_map/all_gather | solution.py:32
  95.2 47.9 %all-to-all-start = ((bf16[16,16,512]{2,0,1:T(8,128)(2,1)}), bf16[16,16,512]{2,0,1:T(8,128)(2,1)S(1)}, u32[]{:S(2)}, u32[]{:S(2)}) async-start(bf16[16,16,512]{2,0,1:T(8,128)(2,1)} %bitcast.8), calls=%async_computation | async-start | bytes 524288 | tf_op jit(solution)/shard_map/all_to_all | solution.py:28
Sparse Core Ops, SparseCore 0:
  94.6 57.9 all-gather.1

commit v2 on v0

--- a/solution.py
+++ b/solution.py
@@ -2,6 +2,12 @@
 import jax.numpy as jnp
 from jax import lax
 from jax.sharding import PartitionSpec as P
+
+
+def gather_and_add(array, axis):
+    blocks = lax.all_gather(array, axis, axis=0, tiled=False)
+    total = blocks.sum(axis=0)
+    return total
 
 
 def on_device(scenarios):
@@ -14,7 +20,7 @@
     block_width = factors // fac_size
     owner_idx = lax.axis_index("scen")
     block_idx = lax.axis_index("fac")
-    col_total = lax.psum(jnp.sum(scenarios.astype(jnp.float32), axis=0), ("scen", "fac"))
+    col_total = gather_and_add(jnp.sum(scenarios.astype(jnp.float32), axis=0), ("scen", "fac"))
     col_mean = col_total / total_rows
     centered = (scenarios.astype(jnp.float32) - col_mean).astype(jnp.bfloat16)
     as_float = centered.astype(jnp.float32)

time: 181 us -> 199 us (1.099)
  waiting for transfers between devices: 10.7 us -> 69.8 us
  blocking collectives: 124 us -> 82 us
    all_gather x0 -> x1, waiting for transfers between devices: none -> 58.9 us  [gather_and_add(): blocks = lax.all_gather(array, axis, axis=0, tiled=False)]
    psum x1 -> x0, blocking collectives: 42.1 us -> none  [on_device(): lax.psum(jnp.sum(scenarios.astype(jnp.float32), axis=0), ('scen', 'fac'))]
  transfers between devices with their start and end apart: 2 -> 3, of which waited for: 1 -> 2; matrix products, arithmetic and copies ran while one was open for 1% -> 1% of each run, Pallas kernels for 0% -> 0%
where the time goes in v2:
time: 199 us; the launch traced here: 198 us
  blocking collectives  82 us (41%)
  waiting for transfers between devices  69.8 us (35%)
  between operations  18.6 us (9%)
  other arithmetic  12.7 us (6%)
  matrix products  6.85 us (3%)
  starting transfers between devices  4.68 us (2%)
  local copies, waits for them, and re-layouts  3.42 us (2%)
    psum x2, blocking collectives, on_device(): lax.psum((trace_part, fourth_part), ('scen', 'fac'))  80.1 us
    all_gather x1, waiting for transfers between devices, gather_and_add(): blocks = lax.all_gather(array, axis, axis=0, tiled=False)  58.9 us
    all_gather x1, waiting for transfers between devices, on_device(): lax.all_gather(wide_cols, 'scen', axis=0, tiled=True)  10.9 us
    add x1, other arithmetic, on_device(): shrunk = (1.0 - shrinkage) * covariance + shrinkage * mu_scale * diag_mask  8.69 us
    dot_general x1, matrix products, on_device(): lax.dot_general(narrow_all, lax.all_gather(wide_cols, 'scen', axis=0, til...  6.85 us
    all_to_all x1, starting transfers between devices, on_device(): lax.all_to_all(local_rows, 'scen', split_axis=1, concat_axis=0, tiled=True)  4.6 us
  transfers between devices with their start and end apart: 3, of which 2 were waited for; matrix products, arithmetic and copies ran while one was open for 1% of the time, Pallas kernels for 0%

profile of v2, /device:TPU:0, one launch (start us, length us, event | category | flops | bytes accessed | tf_op | source)
XLA Modules:
  0.0 198.1 jit_solution(18300053924276771151)
XLA Ops:
  7.2 0.0 all-gather.6.cloned.1.call-start
  7.2 1.6 convert_reduce_fusion
  8.8 0.0 all-gather.6.cloned.1.call-update
  8.8 0.0 all-gather.4.cloned.1.call-start
  8.9 58.9 %all-gather.6.cloned.1.call-done = f32[262144]{0:T(1024)} async-done(((f32[8192]{0:T(1024)}), f32[262144]{0:T(1024)}) %all-gather.6.cloned.1.call-update) | async-done | bytes 1048592 | tf_op jit(solution)/shard_map/all_gather | solution.py:8
  67.8 1.4 reshape.12
  69.2 0.1 reduce_sum.55
  69.3 1.6 fusion.5
  70.9 2.0 %all_gather.14 = bf16[16,8192]{1,0:T(8,128)(2,1)S(1)} all-gather(bf16[8,8192]{1,0:T(8,128)(2,1)S(1)} %get-tuple-element.7), channel_id=1, replica_groups=mesh['scen'=16,'fac'=2] {'fac'}, dimensions={0}, use_global_device_ids=true | all-gather | bytes 393216 | tf_op jit(solution)/shard_map/all_gather | solution.py:32
  72.9 0.7 constant_dynamic-slice_fusion
  73.6 0.0 all-gather.4.cloned.1.call-update
  73.6 0.7 copy.9
  74.3 4.6 %all-to-all-start = ((bf16[16,16,512]{2,0,1:T(8,128)(2,1)}), bf16[16,16,512]{2,0,1:T(8,128)(2,1)S(1)}, u32[]{:S(2)}, u32[]{:S(2)}) async-start(bf16[16,16,512]{2,0,1:T(8,128)(2,1)} %bitcast.8), calls=%async_computation | async-start | bytes 524288 | tf_op jit(solution)/shard_map/all_to_all | solution.py:33
  79.0 41.1 %psum.22 = f32[]{:T(128)} all-reduce(f32[]{:T(128)} %get-tuple-element.3), channel_id=1, replica_groups=mesh['scen'=16,'fac'=2] {'scen','fac'}, use_global_device_ids=true, to_apply=%region_6.0 | all-reduce | flops 1 | bytes 8 | tf_op jit(solution)/shard_map/psum | solution.py:30
  120.1 0.6 dynamic_slice.7
  122.6 0.7 multiply_reduce_fusion
  123.3 0.0 all-to-all-done
  123.3 10.9 %all-gather.4.cloned.1.call-done = bf16[256,4096]{1,0:T(8,128)(2,1)} async-done(((bf16[16,4096]{1,0:T(8,128)(2,1)}), bf16[256,4096]{1,0:T(8,128)(2,1)}) %all-gather.4.cloned.1.call-update) | async-done | bytes 2097168 | tf_op jit(solution)/shard_map/all_gather | solution.py:37
  134.2 6.9 %fusion.2 = (f32[]{:T(128)}, f32[512,4096]{1,0:T(8,128)}) fusion(f32[]{:T(128)S(6)} %div.32, s32[4096]{0:T(1024)S(1)} %iota_add_fusion, s32[512]{0:T(512)S(1)} %iota_add_fusion.1, bf16[256,512]{1,0:T(8,128)(2,1)S(1)} %bitcast.10, bf16[256,4096]{1,0:T(8,128)(2,1)} %all-gather.4.cloned.1.call-done), kind=kOutput, calls=%fused_computation.4 | convolution fusion | flops 1086324736 | bytes 10766344 | tf_op jit(solution)/shard_map/dot_general | solution.py:35
  141.1 38.9 %all-reduce = (f32[]{:T(128)}, f32[]{:T(128)}) all-reduce(f32[]{:T(128)} %multiply_reduce_fusion, f32[]{:T(128)} %get-tuple-element.8), channel_id=1, replica_groups=mesh['scen'=16,'fac'=2] {'scen','fac'}, use_global_device_ids=true, to_apply=%region_4.0 | all-reduce | flops 2 | bytes 16 | tf_op jit(solution)/shard_map/psum | solution.py:30
  181.4 8.7 %fusion.3 = f32[512,4096]{1,0:T(8,128)} fusion(f32[512,4096]{1,0:T(8,128)} %get-tuple-element.9, f32[]{:T(128)S(6)} %mul.61, f32[]{:T(128)S(6)} %mul.58, s32[4096]{0:T(1024)S(1)} %iota_add_fusion, s32[512]{0:T(512)S(1)} %iota_add_fusion.1), kind=kLoop, calls=%fused_computation.5 | loop fusion | flops 8388608 | bytes 16795656 | tf_op jit(solution)/shard_map/add | solution.py:56
  (3 shorter events, 0.0 us)
Async XLA Ops:
  7.2 60.6 %all-gather.6.cloned.1.call-start = ((), (), s32[]{:S(2)}) async-start(), calls=%async_computation.2 | async-start | bytes 1081344 | tf_op jit(solution)/shard_map/all_gather | solution.py:8
  8.8 125.4 %all-gather.4.cloned.1.call-start = ((), (), s32[]{:S(2)}) async-start(), calls=%async_computation.1 | async-start | bytes 2228224 | tf_op jit(solution)/shard_map/all_gather | solution.py:37
  74.3 49.0 %all-to-all-start = ((bf16[16,16,512]{2,0,1:T(8,128)(2,1)}), bf16[16,16,512]{2,0,1:T(8,128)(2,1)S(1)}, u32[]{:S(2)}, u32[]{:S(2)}) async-start(bf16[16,16,512]{2,0,1:T(8,128)(2,1)} %bitcast.8), calls=%async_computation | async-start | bytes 524288 | tf_op jit(solution)/shard_map/all_to_all | solution.py:33
Sparse Core Ops, SparseCore 0:
  11.4 56.3 all-gather.5
  73.7 60.4 all-gather.3

commit v3 on v0

--- a/solution.py
+++ b/solution.py
@@ -2,6 +2,11 @@
 import jax.numpy as jnp
 from jax import lax
 from jax.sharding import PartitionSpec as P
+
+
+def by_each_axis(x, one, other):
+    partial = lax.psum(x, one)
+    return lax.psum(partial, other)
 
 
 def on_device(scenarios):
@@ -21,7 +26,7 @@
     squared = jnp.sum(as_float * as_float, axis=1)
     trace_part = jnp.sum(squared)
     fourth_part = jnp.sum(squared * squared)
-    trace_total, fourth_total = lax.psum((trace_part, fourth_part), ("scen", "fac"))
+    trace_total, fourth_total = by_each_axis((trace_part, fourth_part), "fac", "scen")
     contract = (((0,), (0,)), ((), ()))
     local_rows = lax.all_gather(centered, "fac", axis=0, tiled=True)
     narrow_all = lax.all_to_all(local_rows, "scen", split_axis=1, concat_axis=0, tiled=True)

time: 181 us -> 180 us (level)
  waiting for transfers between devices: 10.7 us -> 4.54 us
  blocking collectives: 124 us -> 130 us
    all_gather x1, waiting for transfers between devices: 10.7 us -> 4.52 us  [on_device(): lax.all_gather(wide_cols, 'scen', axis=0, tiled=True)]
    psum x2 -> x3, blocking collectives: 80.2 us -> 85.7 us  [the longest x1 43.3 us: by_each_axis(): return lax.psum(partial, other)]
where the time goes in v3:
time: 180 us; the launch traced here: 179 us
  blocking collectives  130 us (72%)
  between operations  18.5 us (10%)
  other arithmetic  11.9 us (7%)
  matrix products  6.85 us (4%)
  starting transfers between devices  5.46 us (3%)
  waiting for transfers between devices  4.54 us (3%)
  local copies, waits for them, and re-layouts  2 us (1%)
    psum x1, blocking collectives, by_each_axis(): return lax.psum(partial, other)  43.3 us
    psum x1, blocking collectives, on_device(): lax.psum(jnp.sum(scenarios.astype(jnp.float32), axis=0), ('scen', 'fac'))  42.1 us
    psum x1, blocking collectives, on_device(): frob_sum = lax.psum(jnp.sum(distance * distance), ('scen', 'fac'))  39.4 us
    add x1, other arithmetic, on_device(): shrunk = (1.0 - shrinkage) * covariance + shrinkage * mu_scale * diag_mask  8.69 us
    dot_general x1, matrix products, on_device(): lax.dot_general(narrow_all, lax.all_gather(wide_cols, 'scen', axis=0, til...  6.85 us
    all_to_all x1, starting transfers between devices, on_device(): lax.all_to_all(local_rows, 'scen', split_axis=1, concat_axis=0, tiled=True)  5.42 us
    all_gather x1, waiting for transfers between devices, on_device(): lax.all_gather(wide_cols, 'scen', axis=0, tiled=True)  4.52 us
  transfers between devices with their start and end apart: 2, of which 1 were waited for; matrix products, arithmetic and copies ran while one was open for 1% of the time, Pallas kernels for 0%

profile of v3, /device:TPU:0, one launch (start us, length us, event | category | flops | bytes accessed | tf_op | source)
XLA Modules:
  0.0 179.2 jit_solution(16003750519661413964)
XLA Ops:
  7.2 0.0 all-gather.2.cloned.1.call-start
  7.2 1.0 convert_reduce_fusion
  8.2 42.1 %psum.42 = f32[8192]{0:T(1024)S(1)} all-reduce(f32[8192]{0:T(1024)S(1)} %convert_reduce_fusion), channel_id=1, replica_groups=mesh['scen'=16,'fac'=2] {'scen','fac'}, use_global_device_ids=true, to_apply=%region_1.0 | all-reduce | flops 8192 | bytes 65536 | tf_op jit(solution)/shard_map/psum | solution.py:22
  50.4 1.6 fusion.5
  52.0 2.0 %all_gather.6 = bf16[16,8192]{1,0:T(8,128)(2,1)S(1)} all-gather(bf16[8,8192]{1,0:T(8,128)(2,1)S(1)} %get-tuple-element.9), channel_id=1, replica_groups=mesh['scen'=16,'fac'=2] {'fac'}, dimensions={0}, use_global_device_ids=true | all-gather | bytes 393216 | tf_op jit(solution)/shard_map/all_gather | solution.py:31
  54.0 0.7 constant_dynamic-slice_fusion
  54.6 0.0 all-gather.2.cloned.1.call-update
  54.6 0.7 copy.8
  55.4 5.4 %all-to-all-start = ((bf16[16,16,512]{2,0,1:T(8,128)(2,1)}), bf16[16,16,512]{2,0,1:T(8,128)(2,1)S(1)}, u32[]{:S(2)}, u32[]{:S(2)}) async-start(bf16[16,16,512]{2,0,1:T(8,128)(2,1)} %bitcast.8), calls=%async_computation | async-start | bytes 524288 | tf_op jit(solution)/shard_map/all_to_all | solution.py:32
  60.8 0.6 multiply_reduce_fusion
  61.4 3.1 %all-reduce.1 = (f32[]{:T(128)}, f32[]{:T(128)}) all-reduce(f32[]{:T(128)} %multiply_reduce_fusion, f32[]{:T(128)} %get-tuple-element.3), channel_id=1, replica_groups=mesh['scen'=16,'fac'=2] {'fac'}, use_global_device_ids=true, to_apply=%region_4.0 | all-reduce | flops 2 | bytes 16 | tf_op jit(solution)/shard_map/psum | solution.py:8
  64.5 43.3 %all-reduce = (f32[]{:T(128)}, f32[]{:T(128)}) all-reduce(f32[]{:T(128)} %get-tuple-element.7, f32[]{:T(128)} %get-tuple-element.8), channel_id=1, replica_groups=mesh['scen'=16,'fac'=2] {'scen'}, use_global_device_ids=true, to_apply=%region_5.0 | all-reduce | flops 2 | bytes 16 | tf_op jit(solution)/shard_map/psum | solution.py:9
  107.8 0.6 dynamic_slice.7
  111.0 0.0 all-to-all-done
  111.0 4.5 %all-gather.2.cloned.1.call-done = bf16[256,4096]{1,0:T(8,128)(2,1)} async-done(((bf16[16,4096]{1,0:T(8,128)(2,1)}), bf16[256,4096]{1,0:T(8,128)(2,1)}) %all-gather.2.cloned.1.call-update) | async-done | bytes 2097168 | tf_op jit(solution)/shard_map/all_gather | solution.py:36
  115.6 6.8 %fusion.2 = (f32[]{:T(128)}, f32[512,4096]{1,0:T(8,128)}) fusion(f32[]{:T(128)S(6)} %div.32, s32[4096]{0:T(1024)S(1)} %iota_add_fusion, s32[512]{0:T(512)S(1)} %iota_add_fusion.1, bf16[256,512]{1,0:T(8,128)(2,1)S(1)} %bitcast.10, bf16[256,4096]{1,0:T(8,128)(2,1)} %all-gather.2.cloned.1.call-done), kind=kOutput, calls=%fused_computation.4 | convolution fusion | flops 1086324736 | bytes 10766344 | tf_op jit(solution)/shard_map/dot_general | solution.py:34
  122.4 39.4 %psum.47 = f32[]{:T(128)} all-reduce(f32[]{:T(128)} %get-tuple-element.10), channel_id=1, replica_groups=mesh['scen'=16,'fac'=2] {'scen','fac'}, use_global_device_ids=true, to_apply=%region_10.0 | all-reduce | flops 1 | bytes 8 | tf_op jit(solution)/shard_map/psum | solution.py:50
  162.5 8.7 %fusion.3 = f32[512,4096]{1,0:T(8,128)} fusion(f32[512,4096]{1,0:T(8,128)} %get-tuple-element.11, f32[]{:T(128)S(6)} %mul.61, f32[]{:T(128)S(6)} %mul.58, s32[4096]{0:T(1024)S(1)} %iota_add_fusion, s32[512]{0:T(512)S(1)} %iota_add_fusion.1), kind=kLoop, calls=%fused_computation.5 | loop fusion | flops 8388608 | bytes 16795656 | tf_op jit(solution)/shard_map/add | solution.py:55
  (3 shorter events, 0.0 us)
Async XLA Ops:
  7.2 108.4 %all-gather.2.cloned.1.call-start = ((), (), s32[]{:S(2)}) async-start(), calls=%async_computation.1 | async-start | bytes 2228224 | tf_op jit(solution)/shard_map/all_gather | solution.py:36
  55.4 55.6 %all-to-all-start = ((bf16[16,16,512]{2,0,1:T(8,128)(2,1)}), bf16[16,16,512]{2,0,1:T(8,128)(2,1)S(1)}, u32[]{:S(2)}, u32[]{:S(2)}) async-start(bf16[16,16,512]{2,0,1:T(8,128)(2,1)} %bitcast.8), calls=%async_computation | async-start | bytes 524288 | tf_op jit(solution)/shard_map/all_to_all | solution.py:32
Sparse Core Ops, SparseCore 0:
  54.8 60.7 all-gather.1
